TPU v7x, 32 devices: a whole 2x2x4 slice. The times are simulated.
32 devices in a mesh: vblk: 4 (over y, x), samp: 8 (over z, core).
Axes of the slice: x: 2, y: 2, z: 4, core: 2. Of those that a mesh axis runs over, the one named last changes fastest.
Arguments:
- vectors: bfloat16 [1024, 32768], P('vblk', 'samp'), may hold values from 0 to 2, as said below
- partner: bfloat16 [1024, 32768], P('vblk', 'samp'), may hold values from 0 to 2, as said below
- next_rows: bfloat16 [1024, 32768], P(('vblk', 'samp')), may hold values from 0 to 2, as said below
Outputs:
- metric: float32 [1024, 256], P('vblk', 'samp')
- next_block: bfloat16 [1024, 32768], P('vblk', 'samp')
Inputs may be any that keep to these rules, and one draw needn't show every extreme that they name: vectors: real expected allele dosages, every entry positive. partner: real expected allele dosages, every entry positive. next_rows: real expected allele dosages, every entry positive.
All inputs are finite; a program needn't handle non-finite values.
Results may differ from a plain program's by a relative error of at most 0.0004.
Values may be sent and summed in bfloat16 or wider, within the bound.
No kernel may reach another device: no remote copies, remote signals or barrier semaphores. Data moves between devices by JAX's collectives and lax.ppermute only.
A program may use at most 64 MiB of HBM per device.

v0:
```python
import jax
import jax.numpy as jnp
from jax import lax
from jax.experimental import pallas as pl
from jax.experimental.pallas import tpu as pltpu
from jax.sharding import PartitionSpec as P


F32 = jnp.float32
BF16 = jnp.bfloat16
CUTS = (0, 2, 6, 11, 16)
DEPTH = 8


def from_behind(value, axis, steps):
    count = lax.axis_size(axis)
    pairs = [(source, (source + steps) % count) for source in range(count)]
    return lax.ppermute(value, axis, pairs)


def tree_sum(terms):
    while len(terms) > 1:
        paired = [terms[i] + terms[i + 1] for i in range(0, len(terms) - 1, 2)]
        terms = paired + terms[len(paired) * 2 :]
    return terms[0]


def largest_divisor(size, limit):
    return max(d for d in range(1, limit + 1) if size % d == 0)


def lane_sums(left, right):
    return lax.dot_general(left, right, (((1,), (1,)), ((), ())), preferred_element_type=F32)


def chunk_terms(cols, rows, first, payload, totals, landed):
    col_count, samples = cols.shape
    row_count = rows.shape[0]
    shards, height, _ = payload if isinstance(payload, tuple) else payload.shape
    own = totals[2]
    last = totals[0] is not None
    halves = 2 if samples % 512 == 0 else 1
    span = samples // halves
    depth = largest_divisor(span // 128, DEPTH)
    width = span // depth
    group = 2
    steps = col_count // group
    slot_width = group * halves * width
    chained = not isinstance(payload, tuple)

    def kernel(*refs):
        refs = list(refs)
        col_ref, row_ref = refs[:2]
        refs = refs[2:]
        old_ref = refs.pop(0) if chained else None
        if last:
            row_total_ref, col_total_ref, landed_ref = refs[:3]
            refs = refs[3:]
        out_ref = refs.pop(0)
        if last:
            moved_ref = refs.pop(0)
        wide_ref, part_ref = refs[:2]
        if last:
            move = pltpu.make_async_copy(landed_ref, moved_ref, refs[2])
            move.start()
        wide_ref[...] = col_ref[...].astype(F32)
        if chained:
            out_ref[...] = old_ref[...]
        else:
            out_ref[...] = jnp.zeros_like(out_ref)
        ones = jnp.ones((8, halves * width), BF16)

        def minima(step, slot):
            for half in range(halves):
                start = half * span
                spread = [
                    jnp.broadcast_to(
                        wide_ref[pl.ds(step * group + q, 1), start : start + span], (16, span)
                    ).astype(BF16)
                    for q in range(group)
                ]
                for block in range(0, row_count, 16):
                    for q in range(group):
                        at = slot * slot_width + (q * halves + half) * width
                        part_ref[block : block + 16, at : at + width] = tree_sum(
                            [
                                jnp.minimum(
                                    row_ref[block : block + 16, start + k : start + k + width],
                                    spread[q][:, k : k + width],
                                )
                                for k in range(0, span, width)
                            ]
                        )

        def finish(step, slot):
            for q in range(group):
                at = slot * slot_width + q * halves * width
                line = lane_sums(ones, part_ref[:, at : at + halves * width])
                col = first + step * group + q
                out_ref[col // own, pl.ds(col % own, 1), :] = line[0:1]

        minima(0, 0)

        def two_steps(index, carry):
            finish(2 * index, 0)
            minima(2 * index + 1, 1)
            finish(2 * index + 1, 1)
            minima(jnp.minimum(2 * index + 2, steps - 1), 0)
            return carry

        lax.fori_loop(0, steps // 2, two_steps, 0)
        if last:
            for shard in range(shards):
                out_ref[shard, own : own + 1, :] = row_total_ref[...]
                out_ref[shard, own + 1 : own + 2, :] = col_total_ref[...]
            move.wait()

    vmem = pl.BlockSpec(memory_space=pltpu.VMEM)
    anywhere = pl.BlockSpec(memory_space=pl.ANY)
    operands = [cols, rows] + ([payload] if chained else [])
    in_specs = [vmem] * len(operands)
    out_shape = [jax.ShapeDtypeStruct((shards, height, row_count), F32)]
    out_specs = [vmem]
    scratch = [
        pltpu.VMEM((col_count, samples), F32),
        pltpu.VMEM((row_count, 2 * slot_width), BF16),
    ]
    if last:
        operands += [totals[0], totals[1], landed]
        in_specs += [vmem, vmem, anywhere]
        out_shape.append(jax.ShapeDtypeStruct(landed.shape, landed.dtype))
        out_specs.append(anywhere)
        scratch.append(pltpu.SemaphoreType.DMA(()))
    return pl.pallas_call(
        kernel,
        out_shape=out_shape,
        in_specs=in_specs,
        out_specs=out_specs,
        scratch_shapes=scratch,
        name="chunk_terms",
    )(*operands)


def body(vectors, partner, next_rows):
    shards = lax.axis_size("samp")
    row_count = vectors.shape[0]
    col_count = partner.shape[0]
    own = col_count // shards
    bounds = [col_count * cut // 16 for cut in CUTS]
    arrived = []
    for low, high in zip(bounds, bounds[1:]):
        arrived.append(from_behind(partner[low:high], "vblk", 1))
    samples = next_rows.shape[1] // shards
    outgoing = next_rows.reshape(next_rows.shape[0], shards, samples).transpose(1, 0, 2)
    landed = lax.all_to_all(outgoing, "samp", split_axis=0, concat_axis=0, tiled=True)
    landed = landed.reshape(-1, samples)
    row_totals = jnp.sum(vectors, axis=1, dtype=F32)[None, :]
    col_totals = jnp.sum(partner, axis=1, dtype=F32)[None, :]
    col_totals = from_behind(col_totals, "vblk", 1)
    height = -(-(own + 2) // 8) * 8
    payload = (shards, height, row_count)
    for i, piece in enumerate(arrived):
        last = i == len(arrived) - 1
        totals = (row_totals, col_totals, own) if last else (None, None, own)
        results = chunk_terms(piece, vectors, bounds[i], payload, totals, landed)
        payload = results[0]
    next_block = results[1]
    summed = jnp.sum(
        lax.all_to_all(payload, "samp", split_axis=0, concat_axis=0, tiled=True), axis=0
    )
    mine = lax.dynamic_slice_in_dim(summed[own + 1], lax.axis_index("samp") * own, own)
    metric = 2.0 * summed[:own] / (summed[own][None, :] + mine[:, None])
    return (metric.T, next_block)


def solution(mesh):
    in_specs = (P("vblk", "samp"), P("vblk", "samp"), P(("vblk", "samp"), None))
    out_specs = (P("vblk", "samp"), P("vblk", "samp"))
    return jax.shard_map(body, mesh=mesh, in_specs=in_specs, out_specs=out_specs, check_vma=False)
```

profile of v0, /device:TPU:0, one launch (start us, length us, event | category | flops | bytes accessed | tf_op | source)
XLA Modules:
  0.0 185.6 jit_solution(15671376830510133178)
XLA Ops:
  0.6 3.1 %copy.8 = bf16[4,8,8,4096]{3,2,0,1:T(8,128)(2,1)} copy(bf16[4,8,8,4096]{3,2,1,0:T(8,128)(2,1)} %bitcast.16) | data formatting | bytes 4194304 | tf_op jit(solution)/shard_map/reshape | solution.py:154
  3.8 6.5 %all-to-all-start = ((bf16[8,32,4096]{2,1,0:T(8,128)(2,1)}), bf16[8,32,4096]{2,1,0:T(8,128)(2,1)}, u32[]{:S(2)}, u32[]{:S(2)}) async-start(bf16[8,32,4096]{2,1,0:T(8,128)(2,1)} %bitcast.15), calls=%async_computation | async-start | bytes 4194304 | tf_op jit(solution)/shard_map/all_to_all | solution.py:155
  10.2 0.0 copy-done.1
  10.3 0.0 copy-start.2
  10.3 0.1 fusion.2
  10.4 0.0 copy-start
  10.4 1.5 collective-permute-start.1
  11.9 1.5 collective-permute-start
  13.4 0.8 slice.23
  14.3 1.5 collective-permute-start.2
  15.8 0.5 collective-permute-start.3
  16.3 0.4 convert_reduce_fusion
  16.7 1.5 collective-permute-start.4
  18.2 0.9 convert_reduce_fusion.1
  19.1 40.3 %collective-permute-done.3.refs_0_ = bf16[32,4096]{1,0:T(8,128)(2,1)} collective-permute-done((bf16[32,4096]{1,0:T(8,128)(2,1)S(1)}, bf16[32,4096]{1,0:T(8,128)(2,1)}, u32[]{:S(2)}, u32[]{:S(2)}) %collective-permute-start.3) | collective-permute-done | bytes 262176 | tf_op jit(solution)/shard_map/ppermute | solution.py:18
  59.5 8.4 %chunk_terms.4.refs_2_ = f32[8,40,256]{2,1,0:T(8,128)} custom-call(bf16[32,4096]{1,0:T(8,128)(2,1)} %collective-permute-done.3.refs_0_, bf16[256,4096]{1,0:T(8,128)(2,1)} %refs_1_.7), custom_call_target="tpu_custom_call" | custom-call | tf_op jit(solution)/shard_map/chunk_terms/pallas_call | solution.py:134
  67.9 0.0 collective-permute-done.2.refs_0_
  67.9 0.8 copy-done.5
  68.7 14.2 %chunk_terms.5.refs_2_ = f32[8,40,256]{2,1,0:T(8,128)} custom-call(bf16[64,4096]{1,0:T(8,128)(2,1)} %copy-done.5, bf16[256,4096]{1,0:T(8,128)(2,1)} %refs_1_.7, f32[8,40,256]{2,1,0:T(8,128)} %chunk_terms.4.refs_2_), custom_call_target="tpu_custom_call" | custom-call | tf_op jit(solution)/shard_map/chunk_terms/pallas_call | solution.py:134
  82.9 0.0 collective-permute-done.1.refs_0_
  82.9 0.9 copy-done.4
  83.8 17.1 %chunk_terms.6.refs_2_ = f32[8,40,256]{2,1,0:T(8,128)} custom-call(bf16[80,4096]{1,0:T(8,128)(2,1)} %copy-done.4, bf16[256,4096]{1,0:T(8,128)(2,1)} %refs_1_.7, f32[8,40,256]{2,1,0:T(8,128)} %chunk_terms.5.refs_2_), custom_call_target="tpu_custom_call" | custom-call | tf_op jit(solution)/shard_map/chunk_terms/pallas_call | solution.py:134
  100.9 0.0 collective-permute-done.4.refs_4_
  100.9 0.0 collective-permute-done.refs_0_
  100.9 0.0 all-to-all-done
  100.9 0.6 copy-done.6
  101.5 0.3 copy-done.3
  101.8 67.2 %chunk_terms.7 = (f32[8,40,256]{2,1,0:T(8,128)}, bf16[256,4096]{1,0:T(8,128)(2,1)}) custom-call(bf16[80,4096]{1,0:T(8,128)(2,1)} %copy-done.3, bf16[256,4096]{1,0:T(8,128)(2,1)} %refs_1_.7, f32[8,40,256]{2,1,0:T(8,128)} %chunk_terms.6.refs_2_, f32[1,256]{1,0:T(1,128)} %bitcast.17, f32[1,256]{1,0:T(1,128)} %copy-done.6, bf16[256,4096]{1,0:T(8,128)(2,1)} %bitcast.3.refs_5_), custom_call_target="tpu_custom_call" | custom-call | tf_op jit(solution)/shard_map/chunk_terms/pallas_call | solution.py:134
  168.9 4.7 %all-to-all-start.1 = ((f32[8,40,256]{2,1,0:T(8,128)}), f32[8,40,256]{2,1,0:T(8,128)S(1)}, u32[]{:S(2)}, u32[]{:S(2)}) async-start(f32[8,40,256]{2,1,0:T(8,128)} %get-tuple-element.4), calls=%async_computation.1 | async-start | bytes 655360 | tf_op jit(solution)/shard_map/all_to_all | solution.py:169
  173.7 11.1 %all-to-all-done.1 = f32[8,40,256]{2,1,0:T(8,128)S(1)} async-done(((f32[8,40,256]{2,1,0:T(8,128)}), f32[8,40,256]{2,1,0:T(8,128)S(1)}, u32[]{:S(2)}, u32[]{:S(2)}) %all-to-all-start.1) | async-done | bytes 327712 | tf_op jit(solution)/shard_map/all_to_all | solution.py:169
  184.8 0.1 dynamic-slice_bitcast_fusion
  184.9 0.7 fusion.1
  (10 shorter events, 0.1 us)
Async XLA Ops:
  3.8 6.5 %copy-start.1 = (bf16[256,4096]{1,0:T(8,128)(2,1)S(1)}, bf16[256,4096]{1,0:T(8,128)(2,1)}, u32[]{:S(2)}) copy-start(bf16[256,4096]{1,0:T(8,128)(2,1)} %param.4) | copy-start | bytes 6291460
  3.8 97.2 %all-to-all-start = ((bf16[8,32,4096]{2,1,0:T(8,128)(2,1)}), bf16[8,32,4096]{2,1,0:T(8,128)(2,1)}, u32[]{:S(2)}, u32[]{:S(2)}) async-start(bf16[8,32,4096]{2,1,0:T(8,128)(2,1)} %bitcast.15), calls=%async_computation | async-start | bytes 4194304 | tf_op jit(solution)/shard_map/all_to_all | solution.py:155
  10.3 3.2 %copy-start.2 = (bf16[256,4096]{1,0:T(8,128)(2,1)S(1)}, bf16[256,4096]{1,0:T(8,128)(2,1)}, u32[]{:S(2)}) copy-start(bf16[256,4096]{1,0:T(8,128)(2,1)} %param.4) | copy-start | bytes 6291460
  10.4 7.8 %copy-start = (bf16[256,4096]{1,0:T(8,128)(2,1)S(1)}, bf16[256,4096]{1,0:T(8,128)(2,1)}, u32[]{:S(2)}) copy-start(bf16[256,4096]{1,0:T(8,128)(2,1)} %refs_1_.7) | copy-start | bytes 6291460
  10.4 72.5 %collective-permute-start.1 = (bf16[80,4096]{1,0:T(8,128)(2,1)S(1)}, bf16[80,4096]{1,0:T(8,128)(2,1)S(1)}, u32[]{:S(2)}, u32[]{:S(2)}) collective-permute-start(bf16[80,4096]{1,0:T(8,128)(2,1)S(1)} %get-tuple-element.6), channel_id=1, source_target_pairs={{0,8},{8,16},{16,24},{24,0},{1,9},{9,17},{17,25},{25,1},{2,10},{10... | collective-permute-start | bytes 1966088 | tf_op jit(solution)/shard_map/ppermute | solution.py:18
  11.9 89.0 %collective-permute-start = (bf16[80,4096]{1,0:T(8,128)(2,1)S(1)}, bf16[80,4096]{1,0:T(8,128)(2,1)S(1)}, u32[]{:S(2)}, u32[]{:S(2)}) collective-permute-start(bf16[80,4096]{1,0:T(8,128)(2,1)S(1)} %get-tuple-element.7), channel_id=1, source_target_pairs={{0,8},{8,16},{16,24},{24,0},{1,9},{9,17},{17,25},{25,1},{2,10},{10... | collective-permute-start | bytes 1966088 | tf_op jit(solution)/shard_map/ppermute | solution.py:18
  14.3 53.6 %collective-permute-start.2 = (bf16[64,4096]{1,0:T(8,128)(2,1)}, bf16[64,4096]{1,0:T(8,128)(2,1)S(1)}, u32[]{:S(2)}, u32[]{:S(2)}) collective-permute-start(bf16[64,4096]{1,0:T(8,128)(2,1)} %slice.23), channel_id=1, source_target_pairs={{0,8},{8,16},{16,24},{24,0},{1,9},{9,17},{17,25},{25,1},{2,10},{10... | collective-permute-start | bytes 1572872 | tf_op jit(solution)/shard_map/ppermute | solution.py:18
  15.8 43.7 %collective-permute-start.3 = (bf16[32,4096]{1,0:T(8,128)(2,1)S(1)}, bf16[32,4096]{1,0:T(8,128)(2,1)}, u32[]{:S(2)}, u32[]{:S(2)}) collective-permute-start(bf16[32,4096]{1,0:T(8,128)(2,1)S(1)} %slice.24), channel_id=1, source_target_pairs={{0,8},{8,16},{16,24},{24,0},{1,9},{9,17},{17,25},{25,1},{2,10},{10... | collective-permute-start | bytes 786440 | tf_op jit(solution)/shard_map/ppermute | solution.py:18
  16.7 84.2 %collective-permute-start.4 = (f32[1,256]{1,0:T(1,128)S(1)}, f32[1,256]{1,0:T(1,128)S(1)}, u32[]{:S(2)}, u32[]{:S(2)}) collective-permute-start(f32[1,256]{1,0:T(1,128)S(1)} %bitcast.19), channel_id=1, source_target_pairs={{0,8},{8,16},{16,24},{24,0},{1,9},{9,17},{17,25},{25,1},{2,10},{10... | collective-permute-start | bytes 3080 | tf_op jit(solution)/shard_map/ppermute | solution.py:18
  67.9 0.8 copy-start.5
  82.9 0.9 copy-start.4
  100.9 0.6 copy-start.6
  100.9 0.9 copy-start.3
  168.9 15.8 %all-to-all-start.1 = ((f32[8,40,256]{2,1,0:T(8,128)}), f32[8,40,256]{2,1,0:T(8,128)S(1)}, u32[]{:S(2)}, u32[]{:S(2)}) async-start(f32[8,40,256]{2,1,0:T(8,128)} %get-tuple-element.4), calls=%async_computation.1 | async-start | bytes 655360 | tf_op jit(solution)/shard_map/all_to_all | solution.py:169
where the time goes:
time: 186 us
  Pallas kernels  107 us (58%)
  waiting for transfers between devices  51.5 us (28%)
  starting transfers between devices  17.8 us (10%)
  local copies, waits for them, and re-layouts  6.7 us (4%)
  other arithmetic  2 us (1%)
    pallas_call x4, Pallas kernels, chunk_terms(): pl.pallas_call(kernel, out_shape=out_shape, in_specs=in_specs, out_specs=...  107 us
    ppermute x5, waiting for transfers between devices, from_behind(): return lax.ppermute(value, axis, pairs)  40.4 us
    all_to_all x1, waiting for transfers between devices, body(): lax.all_to_all(payload, 'samp', split_axis=0, concat_axis=0, tiled=True)  11.1 us
    ppermute x5, starting transfers between devices, from_behind(): return lax.ppermute(value, axis, pairs)  6.59 us
    all_to_all x1, starting transfers between devices, body(): lax.all_to_all(outgoing, 'samp', split_axis=0, concat_axis=0, tiled=True)  6.49 us
    all_to_all x1, starting transfers between devices, body(): lax.all_to_all(payload, 'samp', split_axis=0, concat_axis=0, tiled=True)  4.72 us
  transfers between devices with their start and end apart: 7, of which 2 were waited for; matrix products, arithmetic and copies ran while one was open for 1% of the time, Pallas kernels for 21%

commit v1 on v0

--- a/solution.py
+++ b/solution.py
@@ -33,7 +33,7 @@
     return lax.dot_general(left, right, (((1,), (1,)), ((), ())), preferred_element_type=F32)
 
 
-def chunk_terms(cols, rows, first, payload, totals, landed):
+def chunk_terms(cols, rows, first, payload, totals):
     col_count, samples = cols.shape
     row_count = rows.shape[0]
     shards, height, _ = payload if isinstance(payload, tuple) else payload.shape
@@ -54,15 +54,9 @@
         refs = refs[2:]
         old_ref = refs.pop(0) if chained else None
         if last:
-            row_total_ref, col_total_ref, landed_ref = refs[:3]
-            refs = refs[3:]
-        out_ref = refs.pop(0)
-        if last:
-            moved_ref = refs.pop(0)
-        wide_ref, part_ref = refs[:2]
-        if last:
-            move = pltpu.make_async_copy(landed_ref, moved_ref, refs[2])
-            move.start()
+            row_total_ref, col_total_ref = refs[:2]
+            refs = refs[2:]
+        out_ref, wide_ref, part_ref = refs
         wide_ref[...] = col_ref[...].astype(F32)
         if chained:
             out_ref[...] = old_ref[...]
@@ -113,32 +107,42 @@
             for shard in range(shards):
                 out_ref[shard, own : own + 1, :] = row_total_ref[...]
                 out_ref[shard, own + 1 : own + 2, :] = col_total_ref[...]
-            move.wait()
 
     vmem = pl.BlockSpec(memory_space=pltpu.VMEM)
-    anywhere = pl.BlockSpec(memory_space=pl.ANY)
     operands = [cols, rows] + ([payload] if chained else [])
     in_specs = [vmem] * len(operands)
-    out_shape = [jax.ShapeDtypeStruct((shards, height, row_count), F32)]
-    out_specs = [vmem]
     scratch = [
         pltpu.VMEM((col_count, samples), F32),
         pltpu.VMEM((row_count, 2 * slot_width), BF16),
     ]
     if last:
-        operands += [totals[0], totals[1], landed]
-        in_specs += [vmem, vmem, anywhere]
-        out_shape.append(jax.ShapeDtypeStruct(landed.shape, landed.dtype))
-        out_specs.append(anywhere)
-        scratch.append(pltpu.SemaphoreType.DMA(()))
+        operands += [totals[0], totals[1]]
+        in_specs += [vmem, vmem]
     return pl.pallas_call(
         kernel,
-        out_shape=out_shape,
+        out_shape=jax.ShapeDtypeStruct((shards, height, row_count), F32),
         in_specs=in_specs,
-        out_specs=out_specs,
+        out_specs=vmem,
         scratch_shapes=scratch,
         name="chunk_terms",
     )(*operands)
+
+
+def moved(block):
+    rows, samples = block.shape
+    spec = pl.BlockSpec((rows // 8, samples), lambda i: (i, 0))
+
+    def kernel(in_ref, out_ref):
+        out_ref[...] = in_ref[...]
+
+    return pl.pallas_call(
+        kernel,
+        out_shape=jax.ShapeDtypeStruct(block.shape, block.dtype),
+        grid=(8,),
+        in_specs=[spec],
+        out_specs=spec,
+        name="moved",
+    )(block)
 
 
 def body(vectors, partner, next_rows):
@@ -162,12 +166,10 @@
     for i, piece in enumerate(arrived):
         last = i == len(arrived) - 1
         totals = (row_totals, col_totals, own) if last else (None, None, own)
-        results = chunk_terms(piece, vectors, bounds[i], payload, totals, landed)
-        payload = results[0]
-    next_block = results[1]
-    summed = jnp.sum(
-        lax.all_to_all(payload, "samp", split_axis=0, concat_axis=0, tiled=True), axis=0
-    )
+        payload = chunk_terms(piece, vectors, bounds[i], payload, totals)
+    gathered = lax.all_to_all(payload, "samp", split_axis=0, concat_axis=0, tiled=True)
+    next_block = moved(landed)
+    summed = jnp.sum(gathered, axis=0)
     mine = lax.dynamic_slice_in_dim(summed[own + 1], lax.axis_index("samp") * own, own)
     metric = 2.0 * summed[:own] / (summed[own][None, :] + mine[:, None])
     return (metric.T, next_block)

time: 186 us -> 188 us (1.011)
  waiting for transfers between devices: 51.5 us -> 97.3 us
  Pallas kernels: 107 us -> 62.5 us
    all_to_all x1, waiting for transfers between devices: 0.01 us -> 48.1 us  [body(): lax.all_to_all(outgoing, 'samp', split_axis=0, concat_axis=0, tiled=True)]
    pallas_call x4 -> x5, Pallas kernels: 107 us -> 62.5 us  [the longest x4 56.9 us: chunk_terms(): pl.pallas_call(kernel, out_shape=jax.ShapeDtypeStruct((shards, height, ro...]
    all_to_all x1, starting transfers between devices: 6.49 us -> 3.61 us  [body(): lax.all_to_all(outgoing, 'samp', split_axis=0, concat_axis=0, tiled=True)]
    unnamed x14 -> x16, local copies, waits for them, and re-layouts: 2.51 us -> 3.81 us
  transfers between devices with their start and end apart: 7 -> 7, of which waited for: 2 -> 3; matrix products, arithmetic and copies ran while one was open for 1% -> 2% of each run, Pallas kernels for 21% -> 21%
where the time goes in v1:
time: 188 us; the launch traced here: 187 us
  waiting for transfers between devices  97.3 us (52%)
  Pallas kernels  62.5 us (33%)
  starting transfers between devices  16.7 us (9%)
  local copies, waits for them, and re-layouts  7.71 us (4%)
  other arithmetic  2 us (1%)
    pallas_call x4, Pallas kernels, chunk_terms(): pl.pallas_call(kernel, out_shape=jax.ShapeDtypeStruct((shards, height, ro...  56.9 us
    all_to_all x1, waiting for transfers between devices, body(): lax.all_to_all(outgoing, 'samp', split_axis=0, concat_axis=0, tiled=True)  48.1 us
    ppermute x5, waiting for transfers between devices, from_behind(): return lax.ppermute(value, axis, pairs)  39.5 us
    all_to_all x1, waiting for transfers between devices, body(): lax.all_to_all(payload, 'samp', split_axis=0, concat_axis=0, tiled=True)  9.65 us
    ppermute x5, starting transfers between devices, from_behind(): return lax.ppermute(value, axis, pairs)  8.07 us
    pallas_call x1, Pallas kernels, moved(): pl.pallas_call(kernel, out_shape=jax.ShapeDtypeStruct(block.shape, block....  5.63 us
    all_to_all x1, starting transfers between devices, body(): lax.all_to_all(payload, 'samp', split_axis=0, concat_axis=0, tiled=True)  5.07 us
    unnamed x16, local copies, waits for them, and re-layouts  3.81 us
  transfers between devices with their start and end apart: 7, of which 3 were waited for; matrix products, arithmetic and copies ran while one was open for 2% of the time, Pallas kernels for 21%

profile of v1, /device:TPU:0, one launch (start us, length us, event | category | flops | bytes accessed | tf_op | source)
XLA Modules:
  0.0 187.0 jit_solution(14827300023409096502)
XLA Ops:
  0.6 1.5 fusion.2
  2.2 0.0 copy-start
  2.2 3.0 %collective-permute-start.1 = (bf16[80,4096]{1,0:T(8,128)(2,1)S(1)}, bf16[80,4096]{1,0:T(8,128)(2,1)S(1)}, u32[]{:S(2)}, u32[]{:S(2)}) collective-permute-start(bf16[80,4096]{1,0:T(8,128)(2,1)S(1)} %get-tuple-element.2), channel_id=1, source_target_pairs={{0,8},{8,16},{16,24},{24,0},{1,9},{9,17},{17,25},{25,1},{2,10},{10... | collective-permute-start | bytes 1966088 | tf_op jit(solution)/shard_map/ppermute | solution.py:18
  5.2 1.5 collective-permute-start
  6.7 0.8 slice.23
  7.5 1.5 collective-permute-start.2
  9.0 0.1 collective-permute-start.3
  9.1 0.4 convert_reduce_fusion
  9.5 2.0 %collective-permute-start.4 = (f32[1,256]{1,0:T(1,128)S(1)}, f32[1,256]{1,0:T(1,128)S(1)}, u32[]{:S(2)}, u32[]{:S(2)}) collective-permute-start(f32[1,256]{1,0:T(1,128)S(1)} %bitcast.19), channel_id=1, source_target_pairs={{0,8},{8,16},{16,24},{24,0},{1,9},{9,17},{17,25},{25,1},{2,10},{10... | collective-permute-start | bytes 3080 | tf_op jit(solution)/shard_map/ppermute | solution.py:18
  11.5 0.9 convert_reduce_fusion.1
  12.4 39.5 %collective-permute-done.3.refs_0_ = bf16[32,4096]{1,0:T(8,128)(2,1)} collective-permute-done((bf16[32,4096]{1,0:T(8,128)(2,1)S(1)}, bf16[32,4096]{1,0:T(8,128)(2,1)}, u32[]{:S(2)}, u32[]{:S(2)}) %collective-permute-start.3) | collective-permute-done | bytes 262176 | tf_op jit(solution)/shard_map/ppermute | solution.py:18
  51.9 8.4 %chunk_terms.4.refs_2_ = f32[8,40,256]{2,1,0:T(8,128)} custom-call(bf16[32,4096]{1,0:T(8,128)(2,1)} %collective-permute-done.3.refs_0_, bf16[256,4096]{1,0:T(8,128)(2,1)} %refs_1_.7), custom_call_target="tpu_custom_call" | custom-call | tf_op jit(solution)/shard_map/chunk_terms/pallas_call | solution.py:121
  60.3 0.0 collective-permute-done.2.refs_0_
  60.3 0.8 copy-done.6
  61.1 14.2 %chunk_terms.5.refs_2_ = f32[8,40,256]{2,1,0:T(8,128)} custom-call(bf16[64,4096]{1,0:T(8,128)(2,1)} %copy-done.6, bf16[256,4096]{1,0:T(8,128)(2,1)} %refs_1_.7, f32[8,40,256]{2,1,0:T(8,128)} %chunk_terms.4.refs_2_), custom_call_target="tpu_custom_call" | custom-call | tf_op jit(solution)/shard_map/chunk_terms/pallas_call | solution.py:121
  75.3 0.0 collective-permute-done.1.refs_0_
  75.3 0.8 copy-done.5
  76.2 17.1 %chunk_terms.6.refs_2_ = f32[8,40,256]{2,1,0:T(8,128)} custom-call(bf16[80,4096]{1,0:T(8,128)(2,1)} %copy-done.5, bf16[256,4096]{1,0:T(8,128)(2,1)} %refs_1_.7, f32[8,40,256]{2,1,0:T(8,128)} %chunk_terms.5.refs_2_), custom_call_target="tpu_custom_call" | custom-call | tf_op jit(solution)/shard_map/chunk_terms/pallas_call | solution.py:121
  93.3 0.0 collective-permute-done.4.refs_4_
  93.3 0.0 copy-start.4
  93.3 0.5 copy-done.7
  93.8 0.3 copy-done.4
  94.1 17.2 %chunk_terms.7 = f32[8,40,256]{2,1,0:T(8,128)} custom-call(bf16[80,4096]{1,0:T(8,128)(2,1)} %copy-done.4, bf16[256,4096]{1,0:T(8,128)(2,1)} %refs_1_.7, f32[8,40,256]{2,1,0:T(8,128)} %chunk_terms.6.refs_2_, f32[1,256]{1,0:T(1,128)} %bitcast.17, f32[1,256]{1,0:T(1,128)} %copy-done.7), custom_call_target="tpu_custom_call" | custom-call | tf_op jit(solution)/shard_map/chunk_terms/pallas_call | solution.py:121
  111.3 5.1 %all-to-all-start = ((f32[8,40,256]{2,1,0:T(8,128)}), f32[8,40,256]{2,1,0:T(8,128)S(1)}, u32[]{:S(2)}, u32[]{:S(2)}) async-start(f32[8,40,256]{2,1,0:T(8,128)} %chunk_terms.7), calls=%async_computation | async-start | bytes 655360 | tf_op jit(solution)/shard_map/all_to_all | solution.py:170
  116.4 1.5 copy.8
  117.8 9.7 %all-to-all-done = f32[8,40,256]{2,1,0:T(8,128)S(1)} async-done(((f32[8,40,256]{2,1,0:T(8,128)}), f32[8,40,256]{2,1,0:T(8,128)S(1)}, u32[]{:S(2)}, u32[]{:S(2)}) %all-to-all-start) | async-done | bytes 327712 | tf_op jit(solution)/shard_map/all_to_all | solution.py:170
  127.5 3.6 %all-to-all-start.1 = ((bf16[8,32,4096]{2,1,0:T(8,128)(2,1)}), bf16[8,32,4096]{2,1,0:T(8,128)(2,1)S(1)}, u32[]{:S(2)}, u32[]{:S(2)}) async-start(bf16[8,32,4096]{2,1,0:T(8,128)(2,1)} %bitcast.14), calls=%async_computation.1 | async-start | bytes 4194304 | tf_op jit(solution)/shard_map/all_to_all | solution.py:159
  131.1 0.1 dynamic-slice_bitcast_fusion
  131.2 0.7 fusion.1
  131.9 48.1 %all-to-all-done.1 = bf16[8,32,4096]{2,1,0:T(8,128)(2,1)S(1)} async-done(((bf16[8,32,4096]{2,1,0:T(8,128)(2,1)}), bf16[8,32,4096]{2,1,0:T(8,128)(2,1)S(1)}, u32[]{:S(2)}, u32[]{:S(2)}) %all-to-all-start.1) | async-done | bytes 2097184 | tf_op jit(solution)/shard_map/all_to_all | solution.py:159
  180.0 1.3 copy-done.2
  181.4 5.6 %moved.1 = bf16[256,4096]{1,0:T(8,128)(2,1)} custom-call(bf16[256,4096]{1,0:T(8,128)(2,1)} %bitcast.15), custom_call_target="tpu_custom_call" | custom-call | tf_op jit(solution)/shard_map/moved/pallas_call | solution.py:138
  (13 shorter events, 0.1 us)
Async XLA Ops:
  0.6 6.1 %copy-start.1 = (bf16[256,4096]{1,0:T(8,128)(2,1)S(1)}, bf16[256,4096]{1,0:T(8,128)(2,1)}, u32[]{:S(2)}) copy-start(bf16[256,4096]{1,0:T(8,128)(2,1)} %param.4) | copy-start | bytes 6291460
  2.2 9.3 %copy-start = (bf16[256,4096]{1,0:T(8,128)(2,1)S(1)}, bf16[256,4096]{1,0:T(8,128)(2,1)}, u32[]{:S(2)}) copy-start(bf16[256,4096]{1,0:T(8,128)(2,1)} %refs_1_.7) | copy-start | bytes 6291460
  2.2 73.2 %collective-permute-start.1 = (bf16[80,4096]{1,0:T(8,128)(2,1)S(1)}, bf16[80,4096]{1,0:T(8,128)(2,1)S(1)}, u32[]{:S(2)}, u32[]{:S(2)}) collective-permute-start(bf16[80,4096]{1,0:T(8,128)(2,1)S(1)} %get-tuple-element.2), channel_id=1, source_target_pairs={{0,8},{8,16},{16,24},{24,0},{1,9},{9,17},{17,25},{25,1},{2,10},{10... | collective-permute-start | bytes 1966088 | tf_op jit(solution)/shard_map/ppermute | solution.py:18
  5.2 88.1 %collective-permute-start = (bf16[80,4096]{1,0:T(8,128)(2,1)S(1)}, bf16[80,4096]{1,0:T(8,128)(2,1)S(1)}, u32[]{:S(2)}, u32[]{:S(2)}) collective-permute-start(bf16[80,4096]{1,0:T(8,128)(2,1)S(1)} %get-tuple-element.3), channel_id=1, source_target_pairs={{0,8},{8,16},{16,24},{24,0},{1,9},{9,17},{17,25},{25,1},{2,10},{10... | collective-permute-start | bytes 1966088 | tf_op jit(solution)/shard_map/ppermute | solution.py:18
  7.5 52.8 %collective-permute-start.2 = (bf16[64,4096]{1,0:T(8,128)(2,1)}, bf16[64,4096]{1,0:T(8,128)(2,1)S(1)}, u32[]{:S(2)}, u32[]{:S(2)}) collective-permute-start(bf16[64,4096]{1,0:T(8,128)(2,1)} %slice.23), channel_id=1, source_target_pairs={{0,8},{8,16},{16,24},{24,0},{1,9},{9,17},{17,25},{25,1},{2,10},{10... | collective-permute-start | bytes 1572872 | tf_op jit(solution)/shard_map/ppermute | solution.py:18
  9.0 42.9 %collective-permute-start.3 = (bf16[32,4096]{1,0:T(8,128)(2,1)S(1)}, bf16[32,4096]{1,0:T(8,128)(2,1)}, u32[]{:S(2)}, u32[]{:S(2)}) collective-permute-start(bf16[32,4096]{1,0:T(8,128)(2,1)S(1)} %slice.24), channel_id=1, source_target_pairs={{0,8},{8,16},{16,24},{24,0},{1,9},{9,17},{17,25},{25,1},{2,10},{10... | collective-permute-start | bytes 786440 | tf_op jit(solution)/shard_map/ppermute | solution.py:18
  9.5 83.8 %collective-permute-start.4 = (f32[1,256]{1,0:T(1,128)S(1)}, f32[1,256]{1,0:T(1,128)S(1)}, u32[]{:S(2)}, u32[]{:S(2)}) collective-permute-start(f32[1,256]{1,0:T(1,128)S(1)} %bitcast.19), channel_id=1, source_target_pairs={{0,8},{8,16},{16,24},{24,0},{1,9},{9,17},{17,25},{25,1},{2,10},{10... | collective-permute-start | bytes 3080 | tf_op jit(solution)/shard_map/ppermute | solution.py:18
  60.3 0.8 copy-start.6
  75.3 0.8 copy-start.5
  93.3 23.1 %copy-start.3 = (bf16[32,32768]{1,0:T(8,128)(2,1)S(1)}, bf16[32,32768]{1,0:T(8,128)(2,1)}, u32[]{:S(2)}) copy-start(bf16[32,32768]{1,0:T(8,128)(2,1)} %param.5) | copy-start | bytes 6291460
  93.3 0.6 copy-start.7
  93.3 0.8 copy-start.4
  111.3 16.2 %all-to-all-start = ((f32[8,40,256]{2,1,0:T(8,128)}), f32[8,40,256]{2,1,0:T(8,128)S(1)}, u32[]{:S(2)}, u32[]{:S(2)}) async-start(f32[8,40,256]{2,1,0:T(8,128)} %chunk_terms.7), calls=%async_computation | async-start | bytes 655360 | tf_op jit(solution)/shard_map/all_to_all | solution.py:170
  127.5 52.6 %all-to-all-start.1 = ((bf16[8,32,4096]{2,1,0:T(8,128)(2,1)}), bf16[8,32,4096]{2,1,0:T(8,128)(2,1)S(1)}, u32[]{:S(2)}, u32[]{:S(2)}) async-start(bf16[8,32,4096]{2,1,0:T(8,128)(2,1)} %bitcast.14), calls=%async_computation.1 | async-start | bytes 4194304 | tf_op jit(solution)/shard_map/all_to_all | solution.py:159
  180.0 1.3 copy-start.2
